TPU v7x, 256 devices: a whole 4x4x8 slice. The times are simulated.
256 devices in a mesh: rows: 64 (over z, x, core), grp: 4 (over y).
Axes of the slice: x: 4, y: 4, z: 8, core: 2. Of those that a mesh axis runs over, the one named last changes fastest.
Arguments:
- user_features: bfloat16 [4, 16384, 256], P('grp', 'rows'), may hold values from -72 to 72
- w_first: bfloat16 [256, 256], replicated, may hold values from -0.375 to 0.375
- w_second: bfloat16 [256, 256], replicated, may hold values from -0.375 to 0.375
- item_embed: bfloat16 [4, 16384, 256], P('grp', 'rows'), may hold values from -27 to 27
- example_weight: float32 [4, 16384], P('grp', 'rows'), may hold values from 0.02 to 0.2
- positive: int32 [4, 16384], P('grp', 'rows'), may hold values from 0 to 16383
- item_owner: int32 [4, 16384, 1], P('grp', 'rows'), may hold values from 0 to 63; in each aligned block of 256 rows (0 to 255, 256 to 511, ..., all dimensions but the last counted through in order) at most 16 rows name the same one
- item_row: int32 [4, 16384], P('grp', 'rows'), may hold values from 0 to 4095
Outputs:
- grad_first: float32 [256, 256], replicated
- grad_second: float32 [256, 256], replicated
- grad_table: float32 [262144, 256], P('rows', 'grp')
Inputs may be any that keep to these rules, and one draw needn't show every extreme that they name: `item_owner`: within the rows of one device (aligned blocks of 256 pairs of a group) no owner is named by more than 16 pairs, a bound that some block reaches.
All inputs are finite; a program needn't handle non-finite values.
Results may differ from a plain program's by a relative error of at most 0.0023.
The roundings to bfloat16 on the way count: a program that leaves them out, or rounds other values in their place, can miss the bound.
Values may be sent and summed in bfloat16 or wider, within the bound.
A program may use at most 128 MiB of HBM per device.

v0:
```python
import jax
import jax.numpy as jnp
from jax import lax
from jax.sharding import Mesh
from jax.sharding import PartitionSpec as P

ITEMS_DEV = 4096
ROWS = ("rows_0", "rows_1", "rows_2")
ROWS_GRP = ("rows_0", "rows_1", "rows_2", "grp")


def gather_turned(arrays, axis, dims):
    turned = [jnp.moveaxis(a, dim, 0) for a, dim in zip(arrays, dims)]
    widths = [t[0].size for t in turned]
    both = jnp.concatenate([t.reshape(-1, w) for t, w in zip(turned, widths)], axis=1)
    filled = lax.all_gather(both, axis, axis=0, tiled=True)
    tiles = jnp.split(filled, [sum(widths[:k]) for k in range(1, len(widths))], axis=1)
    return tuple(
        (
            jnp.moveaxis(b.reshape(-1, *t.shape[1:]), 0, dim)
            for b, t, dim in zip(tiles, turned, dims)
        )
    )


def cut_along(value, dim, count):
    before, after = (value.shape[:dim], value.shape[dim + 1 :])
    return jnp.moveaxis(value.reshape(*before, count, -1, *after), dim, 0)


def sum_at_owner(value, axis, dim):
    count = lax.axis_size(axis)
    tiles = lax.all_to_all(cut_along(value, dim, count), axis, 0, 0, tiled=True)
    return jnp.sum(tiles, axis=0)


def summed_rows(value, axes, dim):
    far, near = axes
    tiles = cut_along(value, dim, lax.axis_size(far))
    nearer = sum_at_owner(tiles, near, dim + 1)
    arrived = lax.all_to_all(nearer, far, split_axis=0, concat_axis=0, tiled=True)
    return arrived.sum(axis=0)


def padded_to(lines, count):
    spare = -lines.shape[0] % count
    if not spare:
        return lines
    return jnp.concatenate([lines, jnp.zeros((spare, *lines.shape[1:]), lines.dtype)])


def sent_to_all(value, axis):
    count = lax.axis_size(axis)
    return lax.all_to_all(
        jnp.broadcast_to(value[None], (count, *value.shape)), axis, 0, 0, tiled=True
    )


def joined_along(tiles, dim):
    shape = list(tiles.shape[1:])
    shape[dim] *= tiles.shape[0]
    return jnp.moveaxis(tiles, 0, dim).reshape(shape)


def gather_axes(value, axes, dim):
    far, near = axes
    tiles = sent_to_all(sent_to_all(value, far), near)
    return joined_along(tiles.swapaxes(0, 1).reshape(-1, *value.shape), dim)


def total_of(value, axes):
    own = summed_rows(padded_to(value, lax.axis_size(axes[0]) * lax.axis_size(axes[1])), axes, 0)
    whole = gather_axes(own, axes, 0)
    return whole[: len(value)].reshape(value.shape)


def in_one(arrays, axis):
    flat, at, done = (jnp.concatenate([a.reshape(-1) for a in arrays]), 0, [])
    total = total_of(flat, axis)
    for a in arrays:
        done.append(total[at : at + a.size].reshape(a.shape))
        at += a.size
    return tuple(done)


def one_exchange(value, axis, axes, splits, concats):
    sizes = [lax.axis_size(a) for a in axes]
    tiles = cut_along(value, splits[0], sizes[0])
    tiles = jnp.moveaxis(cut_along(tiles, splits[1] + 1, sizes[1]), 0, 1)
    inside = tiles.shape[2:]
    tiles = tiles.reshape(-1, *inside)
    tiles = lax.all_to_all(tiles, axis, split_axis=0, concat_axis=0, tiled=True)
    tiles = joined_along(tiles.reshape(*sizes, *inside), concats[0] + 1)
    return joined_along(tiles, concats[1])


def contract_first(left, right):
    return lax.dot_general(
        left, right, (((0,), (0,)), ((), ())), preferred_element_type=jnp.float32
    )


def contract_last(left, right):
    return lax.dot_general(
        left, right, (((1,), (1,)), ((), ())), preferred_element_type=jnp.float32
    )


def body(
    user_features, w_first, w_second, item_embed, example_weight, positive, item_owner, item_row
):
    features = user_features[0]
    own_items = item_embed[0]
    weights = example_weight[0]
    targets = positive[0]
    owners = item_owner[0, :, 0]
    item_rows = item_row[0]
    my_users = features.shape[0]
    feature_width = own_items.shape[1]
    peers = lax.axis_size(ROWS)
    my_index = lax.axis_index(ROWS)
    pre_act = jnp.dot(features, w_first, preferred_element_type=jnp.float32)
    hidden = jax.nn.silu(pre_act).astype(jnp.bfloat16)
    user_vecs = jnp.dot(hidden, w_second, preferred_element_type=jnp.float32).astype(jnp.bfloat16)
    gathered = lax.all_gather(own_items, ROWS, axis=0, tiled=True)
    group_users = gathered.shape[0]
    scores = contract_last(user_vecs, gathered)
    row_max = jnp.max(scores, axis=1, keepdims=True)
    log_total = row_max + jnp.log(jnp.sum(jnp.exp(scores - row_max), axis=1, keepdims=True))
    columns = lax.broadcasted_iota(jnp.int32, (1, group_users), 1)
    chosen = (columns == targets[:, None]).astype(jnp.float32)
    dscore = (weights[:, None] * (jnp.exp(scores - log_total) - chosen)).astype(jnp.bfloat16)
    grad_user = jnp.dot(dscore, gathered, preferred_element_type=jnp.float32).astype(jnp.bfloat16)
    everyone = lax.all_gather(user_vecs, ROWS, axis=0, tiled=True)
    target_all, total_all, weight_all = gather_turned(
        (targets.astype(jnp.float32), log_total[:, 0], weights), ROWS, (0, 0, 0)
    )
    back_scores = contract_last(everyone, own_items)
    own_columns = my_index * my_users + lax.broadcasted_iota(jnp.int32, (1, my_users), 1)
    hits = (own_columns == target_all.astype(jnp.int32)[:, None]).astype(jnp.float32)
    back_dscore = (weight_all[:, None] * (jnp.exp(back_scores - total_all[:, None]) - hits)).astype(
        jnp.bfloat16
    )
    grad_item = contract_first(back_dscore, everyone)
    d_second = contract_first(hidden, grad_user)
    back_grad = contract_last(grad_user, w_second)
    sigmoid_pre = jax.nn.sigmoid(pre_act)
    grad_pre = (back_grad * sigmoid_pre * (1.0 + pre_act * (1.0 - sigmoid_pre))).astype(
        jnp.bfloat16
    )
    d_first = contract_first(features, grad_pre)
    grad_first, grad_second = in_one((d_first, d_second), (("rows_0", "rows_1"), ("rows_2", "grp")))
    capacity = max(2, 4 * my_users // peers)
    member = (owners[:, None] == lax.broadcasted_iota(jnp.int32, (1, peers), 1)).astype(jnp.int32)
    before = jnp.cumsum(member, axis=0) - member
    slot_rank = jnp.sum(before * member, axis=1)
    slots = owners * capacity + slot_rank
    send_grad = jnp.zeros((peers * capacity, feature_width), jnp.float32).at[slots].set(grad_item)
    send_grad = send_grad.reshape(peers, capacity, feature_width)
    send_rows = (
        jnp.full((peers * capacity,), -1.0, jnp.float32)
        .at[slots]
        .set(item_rows.astype(jnp.float32))
    )
    groups = lax.axis_size("grp")
    rows_wide = jnp.broadcast_to(send_rows.reshape(peers, capacity, 1), (peers, capacity, groups))
    got_grad, got_rows = (
        one_exchange(send_grad, ROWS_GRP, (ROWS, "grp"), (0, 2), (0, 1)),
        one_exchange(rows_wide, ROWS_GRP, (ROWS, "grp"), (0, 2), (0, 1)),
    )
    share_width = feature_width // groups
    table_rows = got_rows.reshape(-1).astype(jnp.int32)
    table_rows = jnp.where(table_rows >= 0, table_rows, ITEMS_DEV)
    grad_table = (
        jnp.zeros((ITEMS_DEV, share_width), jnp.float32)
        .at[table_rows]
        .add(got_grad.reshape(-1, share_width), mode="drop")
    )
    return (grad_first, grad_second, grad_table)


def solution(mesh):
    torus = Mesh(
        mesh.devices.reshape(8, 4, 2, mesh.shape["grp"]), ("rows_0", "rows_1", "rows_2", "grp")
    )
    placed = (
        P("grp", ROWS, None),
        P(),
        P(),
        P("grp", ROWS, None),
        P("grp", ROWS),
        P("grp", ROWS),
        P("grp", ROWS, None),
        P("grp", ROWS),
    )
    return jax.shard_map(
        body, mesh=torus, in_specs=placed, out_specs=(P(), P(), P(ROWS, "grp")), check_vma=False
    )
```

profile of v0, /device:TPU:1, one launch (start us, length us, event | category | flops | bytes accessed | tf_op | source)
XLA Modules:
  0.0 337.8 jit_solution(12011691266853101209)
XLA Ops:
  13.0 84.9 %all-gather.6.cloned.1.call-done = bf16[1,16384,256]{2,1,0:T(8,128)(2,1)} async-done(((bf16[1,256,256]{2,1,0:T(8,128)(2,1)}), bf16[1,16384,256]{2,1,0:T(8,128)(2,1)}) %all-gather.6.cloned.1.call-update) | async-done | bytes 8388624 | tf_op jit(solution)/shard_map/all_gather | solution.py:125
  97.9 11.6 %fusion.36 = (f32[256]{0:T(256)S(1)}, f32[256,16384]{1,0:T(8,128)}) fusion(bf16[256,256]{1,0:T(8,128)(2,1)} %convolution_convert_fusion, bf16[1,16384,256]{2,1,0:T(8,128)(2,1)} %all-gather.6.cloned.1.call-done), kind=kOutput, calls=%fused_computation.61 | convolution fusion | flops 2151677696 | bytes 25297920 | tf_op jit(solution)/shard_map/dot_general | solution.py:104
  109.5 8.3 %exponential_reduce_fusion = f32[256]{0:T(256)S(1)} fusion(f32[256,16384]{1,0:T(8,128)} %get-tuple-element.21, f32[256]{0:T(256)S(1)} %get-tuple-element.20), kind=kLoop, calls=%fused_computation.10 | loop fusion | flops 8388352 | bytes 16779264 | tf_op jit(solution)/shard_map/reduce_sum | solution.py:129
  117.8 13.0 %fusion.11 = bf16[256,256]{1,0:T(8,128)(2,1)S(1)} fusion(bf16[1,16384,256]{2,1,0:T(8,128)(2,1)} %all-gather.6.cloned.1.call-done, f32[256,16384]{1,0:T(8,128)} %get-tuple-element.21, s32[256]{0:T(256)S(1)} %bitcast.120, f32[256]{0:T(256)S(1)} %log_add_fusion, f32[256]{0:T(256)S(1)} %bitcast.116), kind=kOutput, calls=%fused_computation.21 | convolution fusion | flops 2172715008 | bytes 25299968 | tf_op jit(solution)/shard_map/dot_general | solution.py:133
  133.1 4.5 %all-to-all-start = ((f32[8,32,512]{2,1,0:T(8,128)}), f32[8,32,512]{2,1,0:T(8,128)S(1)}, u32[]{:S(2)}, u32[]{:S(2)}) async-start(f32[8,32,512]{2,1,0:T(8,128)} %copy.25), calls=%async_computation | async-start | bytes 1048576 | tf_op jit(solution)/shard_map/all_to_all | solution.py:33
  137.6 1.4 scatter_custom_fusion
  139.1 7.8 %all-to-all-done = f32[8,32,512]{2,1,0:T(8,128)S(1)} async-done(((f32[8,32,512]{2,1,0:T(8,128)}), f32[8,32,512]{2,1,0:T(8,128)S(1)}, u32[]{:S(2)}, u32[]{:S(2)}) %all-to-all-start) | async-done | bytes 524320 | tf_op jit(solution)/shard_map/all_to_all | solution.py:33
  147.7 5.1 %all-to-all-start.1 = ((f32[32,1,512]{2,1,0:T(1,128)}), f32[32,1,512]{2,1,0:T(1,128)S(1)}, u32[]{:S(2)}, u32[]{:S(2)}) async-start(f32[32,1,512]{2,1,0:T(1,128)} %all_to_all.23), calls=%async_computation.1 | async-start | bytes 131072 | tf_op jit(solution)/shard_map/all_to_all | solution.py:41
  152.8 45.7 %all_gather.10 = f32[16384,3]{0,1:T(4,128)S(1)} all-gather(f32[256,3]{0,1:T(4,128)S(1)} %pad_maximum_fusion), channel_id=1, replica_groups=mesh['rows_0'=8,'rows_1'=4,'rows_2'=2,'grp'=4] {'rows_0','rows_1','rows_2'}, dimensions={0}, use_global_device_ids=true | all-gather | bytes 199680 | tf_op jit(solution)/shard_map/all_gather | solution.py:16
  199.2 6.6 %all-to-all-start.2 = ((f32[32,1,512]{2,1,0:T(1,128)}), f32[32,1,512]{2,1,0:T(1,128)S(1)}, u32[]{:S(2)}, u32[]{:S(2)}) async-start(f32[32,1,512]{2,1,0:T(1,128)} %broadcast_in_dim.17), calls=%async_computation.2 | async-start | bytes 131072 | tf_op jit(solution)/shard_map/all_to_all | solution.py:54
  206.0 8.7 %all-to-all-done.2 = f32[32,1,512]{2,1,0:T(1,128)S(1)} async-done(((f32[32,1,512]{2,1,0:T(1,128)}), f32[32,1,512]{2,1,0:T(1,128)S(1)}, u32[]{:S(2)}, u32[]{:S(2)}) %all-to-all-start.2) | async-done | bytes 65568 | tf_op jit(solution)/shard_map/all_to_all | solution.py:54
  215.4 6.6 %all-to-all-start.4 = ((f32[256,1,16,1]{2,3,1,0:T(1,128)}), f32[256,1,16,1]{2,3,1,0:T(1,128)S(1)}, u32[]{:S(2)}, u32[]{:S(2)}) async-start(f32[256,1,16,1]{2,3,1,0:T(1,128)} %bitcast.14), calls=%async_computation.4 | async-start | bytes 262144 | tf_op jit(solution)/shard_map/all_to_all | solution.py:92
  222.0 12.5 %fusion.3.clone.4 = bf16[16384,256]{1,0:T(8,128)(2,1)} fusion(bf16[16384,256]{1,0:T(8,128)(2,1)} %all-gather.4.cloned.1.call-done, s32[256]{0:T(256)S(1)} %iota_add_fusion, f32[16384]{0:T(1024)S(1)} %bitcast.109, f32[16384]{0:T(1024)S(1)} %bitcast.110, s32[16384]{0:T(1024)S(1)} %bitcast.108, bf16[1,256,256]{2,1,0:T(8,128)(2,1)S(1)} %copy-done.1), kind=kOutput, calls=%fused_computation.7.clone.clone.clone.1 | convolution fusion | flops 2172649472 | bytes 17105920 | tf_op jit(solution)/shard_map/dot_general | solution.py:104
  235.7 6.1 %all-to-all-start.3 = ((f32[8,32,512]{2,1,0:T(8,128)}), f32[8,32,512]{2,1,0:T(8,128)}, u32[]{:S(2)}, u32[]{:S(2)}) async-start(f32[8,32,512]{2,1,0:T(8,128)} %broadcast_in_dim.19), calls=%async_computation.3 | async-start | bytes 1048576 | tf_op jit(solution)/shard_map/all_to_all | solution.py:54
  241.8 8.1 %fusion.8 = f32[256,256]{1,0:T(8,128)S(1)} fusion(bf16[16384,256]{1,0:T(8,128)(2,1)} %all-gather.4.cloned.1.call-done, bf16[16384,256]{1,0:T(8,128)(2,1)} %fusion.3.clone.4), kind=kOutput, calls=%fused_computation.15 | convolution fusion | flops 2147483648 | bytes 17039360 | tf_op jit(solution)/shard_map/dot_general | solution.py:98
  249.9 1.7 scatter_custom_fusion.1
  252.5 1.5 copy.29
  254.0 3.4 %reshape.203 = f32[256,1,1024]{2,1,0:T(1,128)} reshape(f32[256,1,16,64]{3,2,1,0:T(8,128)} %bitcast.104) | data formatting | bytes 2097152
  257.5 12.3 %all-to-all-start.5 = ((f32[256,1,1024]{2,1,0:T(1,128)}), f32[256,1,1024]{2,1,0:T(1,128)S(1)}, u32[]{:S(2)}, u32[]{:S(2)}) async-start(f32[256,1,1024]{2,1,0:T(1,128)} %reshape.203), calls=%async_computation.5 | async-start | bytes 2097152 | tf_op jit(solution)/shard_map/all_to_all | solution.py:92
  273.0 27.7 %all-to-all-done.5 = f32[256,1,1024]{2,1,0:T(1,128)S(1)} async-done(((f32[256,1,1024]{2,1,0:T(1,128)}), f32[256,1,1024]{2,1,0:T(1,128)S(1)}, u32[]{:S(2)}, u32[]{:S(2)}) %all-to-all-start.5) | async-done | bytes 1048608 | tf_op jit(solution)/shard_map/all_to_all | solution.py:92
  301.2 3.1 reduce.3
  304.3 1.9 reshape.204
  306.2 23.2 %scatter_custom_fusion.2 = f32[4096,64]{1,0:T(8,128)S(1)} fusion(s32[4096]{0:T(1024)S(1)} %bitcast.111, f32[4096,64]{1,0:T(8,128)} %bitcast.105, f32[]{:T(128)} %constant.18.clone.1), kind=kCustom, calls=%fused_computation.22 | custom fusion | flops 262144 | bytes 1049088 | tf_op jit(solution)/shard_map/scatter-add | solution.py:177
  329.4 1.6 copy.31
  (60 shorter events, 16.1 us)
Async XLA Ops:
  7.2 2.0 copy-start
  7.2 90.7 %all-gather.6.cloned.1.call-start = ((), (), s32[]{:S(2)}) async-start(), calls=%async_computation.7 | async-start | bytes 8519680 | tf_op jit(solution)/shard_map/all_gather | solution.py:125
  7.9 214.1 %all-gather.4.cloned.1.call-start = ((), (), s32[]{:S(2)}) async-start(), calls=%async_computation.6 | async-start | bytes 8519680 | tf_op jit(solution)/shard_map/all_gather | solution.py:134
  109.5 8.3 %copy-start.4 = (f32[1,256]{1,0:T(1,128)S(1)}, f32[1,256]{1,0:T(1,128)}, u32[]{:S(2)}) copy-start(f32[1,256]{1,0:T(1,128)} %param.12) | copy-start | bytes 3076
  109.5 8.3 %copy-start.5 = (s32[1,256]{1,0:T(1,128)S(1)}, s32[1,256]{1,0:T(1,128)}, u32[]{:S(2)}) copy-start(s32[1,256]{1,0:T(1,128)} %param.13) | copy-start | bytes 3076
  117.8 13.4 %copy-start.2 = (bf16[1,256,256]{2,1,0:T(8,128)(2,1)S(1)}, bf16[1,256,256]{2,1,0:T(8,128)(2,1)}, u32[]{:S(2)}) copy-start(bf16[1,256,256]{2,1,0:T(8,128)(2,1)} %param.8) | copy-start | bytes 393220
  117.8 19.8 %copy-start.3 = (s32[1,256,1]{1,2,0:T(1,128)S(1)}, s32[1,256,1]{1,2,0:T(1,128)}, u32[]{:S(2)}) copy-start(s32[1,256,1]{1,2,0:T(1,128)} %param.14) | copy-start | bytes 3076
  130.9 91.1 %copy-start.1 = (bf16[1,256,256]{2,1,0:T(8,128)(2,1)S(1)}, bf16[1,256,256]{2,1,0:T(8,128)(2,1)}, u32[]{:S(2)}) copy-start(bf16[1,256,256]{2,1,0:T(8,128)(2,1)} %param.11) | copy-start | bytes 393220
  133.1 13.9 %all-to-all-start = ((f32[8,32,512]{2,1,0:T(8,128)}), f32[8,32,512]{2,1,0:T(8,128)S(1)}, u32[]{:S(2)}, u32[]{:S(2)}) async-start(f32[8,32,512]{2,1,0:T(8,128)} %copy.25), calls=%async_computation | async-start | bytes 1048576 | tf_op jit(solution)/shard_map/all_to_all | solution.py:33
  147.7 50.8 %all-to-all-start.1 = ((f32[32,1,512]{2,1,0:T(1,128)}), f32[32,1,512]{2,1,0:T(1,128)S(1)}, u32[]{:S(2)}, u32[]{:S(2)}) async-start(f32[32,1,512]{2,1,0:T(1,128)} %all_to_all.23), calls=%async_computation.1 | async-start | bytes 131072 | tf_op jit(solution)/shard_map/all_to_all | solution.py:41
  199.2 15.5 %all-to-all-start.2 = ((f32[32,1,512]{2,1,0:T(1,128)}), f32[32,1,512]{2,1,0:T(1,128)S(1)}, u32[]{:S(2)}, u32[]{:S(2)}) async-start(f32[32,1,512]{2,1,0:T(1,128)} %broadcast_in_dim.17), calls=%async_computation.2 | async-start | bytes 131072 | tf_op jit(solution)/shard_map/all_to_all | solution.py:54
  215.4 19.4 %all-to-all-start.4 = ((f32[256,1,16,1]{2,3,1,0:T(1,128)}), f32[256,1,16,1]{2,3,1,0:T(1,128)S(1)}, u32[]{:S(2)}, u32[]{:S(2)}) async-start(f32[256,1,16,1]{2,3,1,0:T(1,128)} %bitcast.14), calls=%async_computation.4 | async-start | bytes 262144 | tf_op jit(solution)/shard_map/all_to_all | solution.py:92
  235.7 21.8 %all-to-all-start.3 = ((f32[8,32,512]{2,1,0:T(8,128)}), f32[8,32,512]{2,1,0:T(8,128)}, u32[]{:S(2)}, u32[]{:S(2)}) async-start(f32[8,32,512]{2,1,0:T(8,128)} %broadcast_in_dim.19), calls=%async_computation.3 | async-start | bytes 1048576 | tf_op jit(solution)/shard_map/all_to_all | solution.py:54
  257.5 43.2 %all-to-all-start.5 = ((f32[256,1,1024]{2,1,0:T(1,128)}), f32[256,1,1024]{2,1,0:T(1,128)S(1)}, u32[]{:S(2)}, u32[]{:S(2)}) async-start(f32[256,1,1024]{2,1,0:T(1,128)} %reshape.203), calls=%async_computation.5 | async-start | bytes 2097152 | tf_op jit(solution)/shard_map/all_to_all | solution.py:92
Sparse Core Ops, SparseCore 0:
  10.8 87.1 all-gather.5
  101.3 79.9 all-gather.3
where the time goes:
time: 338 us
  waiting for transfers between devices  130 us (38%)
  matrix products  48 us (14%)
  blocking collectives  45.7 us (14%)
  starting transfers between devices  41.3 us (12%)
  other arithmetic  37.8 us (11%)
  local copies, waits for them, and re-layouts  20.6 us (6%)
  between operations  14.3 us (4%)
    all_gather x1, waiting for transfers between devices, body(): gathered = lax.all_gather(own_items, ROWS, axis=0, tiled=True)  84.9 us
    all_gather x1, blocking collectives, gather_turned(): filled = lax.all_gather(both, axis, axis=0, tiled=True)  45.7 us
    all_to_all x2, waiting for transfers between devices, one_exchange(): tiles = lax.all_to_all(tiles, axis, split_axis=0, concat_axis=0, tiled=True)  27.9 us
    dot_general x2, matrix products, contract_last(): lax.dot_general(left, right, (((1,), (1,)), ((), ())), preferred_element_...  24.1 us
    scatter-add x1, other arithmetic, body(): grad_table = jnp.zeros((ITEMS_DEV, share_width), jnp.float32).at[table_ro...  23.2 us
    all_to_all x2, starting transfers between devices, one_exchange(): tiles = lax.all_to_all(tiles, axis, split_axis=0, concat_axis=0, tiled=True)  18.9 us
    dot_general x1, matrix products, body(): jnp.dot(dscore, gathered, preferred_element_type=jnp.float32)  13 us
    all_to_all x2, starting transfers between devices, sent_to_all(): lax.all_to_all(jnp.broadcast_to(value[None], (count, *value.shape)), axis...  12.7 us
  transfers between devices with their start and end apart: 8, of which 5 were waited for; matrix products, arithmetic and copies ran while one was open for 22% of the time, Pallas kernels for 0%

commit v1 on v0

--- a/solution.py
+++ b/solution.py
@@ -122,7 +122,9 @@
     pre_act = jnp.dot(features, w_first, preferred_element_type=jnp.float32)
     hidden = jax.nn.silu(pre_act).astype(jnp.bfloat16)
     user_vecs = jnp.dot(hidden, w_second, preferred_element_type=jnp.float32).astype(jnp.bfloat16)
-    gathered = lax.all_gather(own_items, ROWS, axis=0, tiled=True)
+    gathered = jnp.concatenate(
+        lax.all_to_all(jnp.stack([own_items] * lax.axis_size(ROWS)), ROWS, 0, 0), axis=0
+    )
     group_users = gathered.shape[0]
     scores = contract_last(user_vecs, gathered)
     row_max = jnp.max(scores, axis=1, keepdims=True)

time: 338 us -> 477 us (1.41)
  waiting for transfers between devices: 130 us -> 249 us
  starting transfers between devices: 41.3 us -> 59 us
  local copies, waits for them, and re-layouts: 20.6 us -> 25.8 us
    all_to_all x0 -> x1, waiting for transfers between devices: none -> 205 us  [body(): lax.all_to_all(jnp.stack([own_items] * lax.axis_size(ROWS)), ROWS, 0, 0)]
    all_gather x1 -> x0, waiting for transfers between devices: 84.9 us -> none  [body(): gathered = lax.all_gather(own_items, ROWS, axis=0, tiled=True)]
    all_to_all x0 -> x1, starting transfers between devices: none -> 13.3 us  [body(): lax.all_to_all(jnp.stack([own_items] * lax.axis_size(ROWS)), ROWS, 0, 0)]
    another operation x1 -> x2, local copies, waits for them, and re-layouts: 0.01 us -> 5.18 us  [the longest x1 5.17 us: body(): jnp.stack([own_items] * lax.axis_size(ROWS))]
  transfers between devices with their start and end apart: 8 -> 8, of which waited for: 5 -> 5; matrix products, arithmetic and copies ran while one was open for 22% -> 15% of each run, Pallas kernels for 0% -> 0%
where the time goes in v1:
time: 477 us; the launch traced here: 476 us
  waiting for transfers between devices  249 us (52%)
  starting transfers between devices  59 us (12%)
  matrix products  46.9 us (10%)
  blocking collectives  45.4 us (10%)
  other arithmetic  35.6 us (7%)
  local copies, waits for them, and re-layouts  25.8 us (5%)
  between operations  14.4 us (3%)
    all_to_all x1, waiting for transfers between devices, body(): lax.all_to_all(jnp.stack([own_items] * lax.axis_size(ROWS)), ROWS, 0, 0)  205 us
    all_gather x1, blocking collectives, gather_turned(): filled = lax.all_gather(both, axis, axis=0, tiled=True)  45.4 us
    all_to_all x2, waiting for transfers between devices, one_exchange(): tiles = lax.all_to_all(tiles, axis, split_axis=0, concat_axis=0, tiled=True)  27.9 us
    dot_general x2, matrix products, contract_last(): lax.dot_general(left, right, (((1,), (1,)), ((), ())), preferred_element_...  24.1 us
    scatter-add x1, other arithmetic, body(): grad_table = jnp.zeros((ITEMS_DEV, share_width), jnp.float32).at[table_ro...  23.2 us
    all_to_all x2, starting transfers between devices, one_exchange(): tiles = lax.all_to_all(tiles, axis, split_axis=0, concat_axis=0, tiled=True)  18.9 us
    all_to_all x1, starting transfers between devices, body(): lax.all_to_all(jnp.stack([own_items] * lax.axis_size(ROWS)), ROWS, 0, 0)  13.3 us
    dot_general x1, matrix products, body(): jnp.dot(dscore, gathered, preferred_element_type=jnp.float32)  12.9 us
  transfers between devices with their start and end apart: 8, of which 5 were waited for; matrix products, arithmetic and copies ran while one was open for 15% of the time, Pallas kernels for 0%

profile of v1, /device:TPU:1, one launch (start us, length us, event | category | flops | bytes accessed | tf_op | source)
XLA Modules:
  0.0 476.4 jit_solution(4701458576502261874)
XLA Ops:
  7.2 5.2 %stack.3 = bf16[64,256,256]{2,1,0:T(8,128)(2,1)} broadcast(bf16[256,256]{1,0:T(8,128)(2,1)} %bitcast.102), dimensions={1,2} | broadcast | bytes 8519680 | tf_op jit(solution)/shard_map/stack | solution.py:126
  12.4 13.3 %all-to-all-start = ((bf16[64,256,256]{2,1,0:T(8,128)(2,1)}), bf16[64,256,256]{2,1,0:T(8,128)(2,1)}, u32[]{:S(2)}, u32[]{:S(2)}) async-start(bf16[64,256,256]{2,1,0:T(8,128)(2,1)} %stack.3), calls=%async_computation | async-start | bytes 16777216 | tf_op jit(solution)/shard_map/all_to_all | solution.py:126
  27.8 204.8 %all-to-all-done = bf16[64,256,256]{2,1,0:T(8,128)(2,1)} async-done(((bf16[64,256,256]{2,1,0:T(8,128)(2,1)}), bf16[64,256,256]{2,1,0:T(8,128)(2,1)}, u32[]{:S(2)}, u32[]{:S(2)}) %all-to-all-start) | async-done | bytes 8388640 | tf_op jit(solution)/shard_map/all_to_all | solution.py:126
  232.7 11.6 %fusion.31 = (f32[256]{0:T(256)S(1)}, f32[256,16384]{1,0:T(8,128)}) fusion(bf16[256,256]{1,0:T(8,128)(2,1)} %convolution_convert_fusion, bf16[16384,256]{1,0:T(8,128)(2,1)} %bitcast.3), kind=kOutput, calls=%fused_computation.58 | convolution fusion | flops 2151677696 | bytes 25297920 | tf_op jit(solution)/shard_map/dot_general | solution.py:104
  244.2 8.2 %exponential_reduce_fusion = f32[256]{0:T(256)S(1)} fusion(f32[256,16384]{1,0:T(8,128)} %get-tuple-element.21, f32[256]{0:T(256)S(1)} %get-tuple-element.20), kind=kLoop, calls=%fused_computation.10 | loop fusion | flops 8388352 | bytes 16779264 | tf_op jit(solution)/shard_map/reduce_sum | solution.py:131
  252.4 12.9 %fusion.8 = bf16[256,256]{1,0:T(8,128)(2,1)S(1)} fusion(bf16[16384,256]{1,0:T(8,128)(2,1)} %bitcast.3, f32[256,16384]{1,0:T(8,128)} %get-tuple-element.21, s32[256]{0:T(256)S(1)} %bitcast.115, f32[256]{0:T(256)S(1)} %log_add_fusion, f32[256]{0:T(256)S(1)} %bitcast.111), kind=kOutput, calls=%fused_computation.18 | convolution fusion | flops 2172715008 | bytes 25299968 | tf_op jit(solution)/shard_map/dot_general | solution.py:135
  267.6 8.6 %all-to-all-start.1 = ((f32[8,32,512]{2,1,0:T(8,128)}), f32[8,32,512]{2,1,0:T(8,128)S(1)}, u32[]{:S(2)}, u32[]{:S(2)}) async-start(f32[8,32,512]{2,1,0:T(8,128)} %copy.25), calls=%async_computation.1 | async-start | bytes 1048576 | tf_op jit(solution)/shard_map/all_to_all | solution.py:33
  277.6 7.8 %all-to-all-done.1 = f32[8,32,512]{2,1,0:T(8,128)S(1)} async-done(((f32[8,32,512]{2,1,0:T(8,128)}), f32[8,32,512]{2,1,0:T(8,128)S(1)}, u32[]{:S(2)}, u32[]{:S(2)}) %all-to-all-start.1) | async-done | bytes 524320 | tf_op jit(solution)/shard_map/all_to_all | solution.py:33
  286.2 5.4 %all-to-all-start.2 = ((f32[32,1,512]{2,1,0:T(1,128)}), f32[32,1,512]{2,1,0:T(1,128)S(1)}, u32[]{:S(2)}, u32[]{:S(2)}) async-start(f32[32,1,512]{2,1,0:T(1,128)} %all_to_all.27), calls=%async_computation.2 | async-start | bytes 131072 | tf_op jit(solution)/shard_map/all_to_all | solution.py:41
  291.6 45.4 %all_gather.6 = f32[16384,3]{0,1:T(4,128)S(1)} all-gather(f32[256,3]{0,1:T(4,128)S(1)} %pad_maximum_fusion), channel_id=1, replica_groups=mesh['rows_0'=8,'rows_1'=4,'rows_2'=2,'grp'=4] {'rows_0','rows_1','rows_2'}, dimensions={0}, use_global_device_ids=true | all-gather | bytes 199680 | tf_op jit(solution)/shard_map/all_gather | solution.py:16
  337.7 6.7 %all-to-all-start.3 = ((f32[32,1,512]{2,1,0:T(1,128)}), f32[32,1,512]{2,1,0:T(1,128)S(1)}, u32[]{:S(2)}, u32[]{:S(2)}) async-start(f32[32,1,512]{2,1,0:T(1,128)} %broadcast_in_dim.17), calls=%async_computation.3 | async-start | bytes 131072 | tf_op jit(solution)/shard_map/all_to_all | solution.py:54
  344.6 8.7 %all-to-all-done.3 = f32[32,1,512]{2,1,0:T(1,128)S(1)} async-done(((f32[32,1,512]{2,1,0:T(1,128)}), f32[32,1,512]{2,1,0:T(1,128)S(1)}, u32[]{:S(2)}, u32[]{:S(2)}) %all-to-all-start.3) | async-done | bytes 65568 | tf_op jit(solution)/shard_map/all_to_all | solution.py:54
  354.0 6.6 %all-to-all-start.5 = ((f32[256,1,16,1]{2,3,1,0:T(1,128)}), f32[256,1,16,1]{2,3,1,0:T(1,128)S(1)}, u32[]{:S(2)}, u32[]{:S(2)}) async-start(f32[256,1,16,1]{2,3,1,0:T(1,128)} %bitcast.15), calls=%async_computation.5 | async-start | bytes 262144 | tf_op jit(solution)/shard_map/all_to_all | solution.py:92
  360.6 12.5 %fusion.3.clone.4 = bf16[16384,256]{1,0:T(8,128)(2,1)} fusion(bf16[16384,256]{1,0:T(8,128)(2,1)} %all-gather.2.cloned.1.call-done, s32[256]{0:T(256)S(1)} %iota_add_fusion, f32[16384]{0:T(1024)S(1)} %bitcast.104, f32[16384]{0:T(1024)S(1)} %bitcast.105, s32[16384]{0:T(1024)S(1)} %bitcast.103, bf16[1,256,256]{2,1,0:T(8,128)(2,1)S(1)} %copy-done.2), kind=kOutput, calls=%fused_computation.7.clone.clone.clone.1 | convolution fusion | flops 2172649472 | bytes 17105920 | tf_op jit(solution)/shard_map/dot_general | solution.py:104
  374.3 6.1 %all-to-all-start.4 = ((f32[8,32,512]{2,1,0:T(8,128)}), f32[8,32,512]{2,1,0:T(8,128)}, u32[]{:S(2)}, u32[]{:S(2)}) async-start(f32[8,32,512]{2,1,0:T(8,128)} %broadcast_in_dim.19), calls=%async_computation.4 | async-start | bytes 1048576 | tf_op jit(solution)/shard_map/all_to_all | solution.py:54
  380.4 8.1 %fusion.5 = f32[256,256]{1,0:T(8,128)S(1)} fusion(bf16[16384,256]{1,0:T(8,128)(2,1)} %all-gather.2.cloned.1.call-done, bf16[16384,256]{1,0:T(8,128)(2,1)} %fusion.3.clone.4), kind=kOutput, calls=%fused_computation.12 | convolution fusion | flops 2147483648 | bytes 17039360 | tf_op jit(solution)/shard_map/dot_general | solution.py:98
  388.5 1.7 scatter_custom_fusion.1
  392.6 3.5 reshape.207
  396.1 12.3 %all-to-all-start.6 = ((f32[256,1,1024]{2,1,0:T(1,128)}), f32[256,1,1024]{2,1,0:T(1,128)S(1)}, u32[]{:S(2)}, u32[]{:S(2)}) async-start(f32[256,1,1024]{2,1,0:T(1,128)} %reshape.207), calls=%async_computation.6 | async-start | bytes 2097152 | tf_op jit(solution)/shard_map/all_to_all | solution.py:92
  411.6 27.7 %all-to-all-done.6 = f32[256,1,1024]{2,1,0:T(1,128)S(1)} async-done(((f32[256,1,1024]{2,1,0:T(1,128)}), f32[256,1,1024]{2,1,0:T(1,128)S(1)}, u32[]{:S(2)}, u32[]{:S(2)}) %all-to-all-start.6) | async-done | bytes 1048608 | tf_op jit(solution)/shard_map/all_to_all | solution.py:92
  439.8 3.1 reduce.3
  442.9 1.9 reshape.208
  444.8 23.2 %scatter_custom_fusion.2 = f32[4096,64]{1,0:T(8,128)S(1)} fusion(s32[4096]{0:T(1024)S(1)} %bitcast.106, f32[4096,64]{1,0:T(8,128)} %bitcast.99, f32[]{:T(128)} %constant.18.clone.1), kind=kCustom, calls=%fused_computation.19 | custom fusion | flops 262144 | bytes 1049088 | tf_op jit(solution)/shard_map/scatter-add | solution.py:179
  468.0 1.6 copy.31
  (66 shorter events, 15.3 us)
Async XLA Ops:
  7.2 18.8 %copy-start = (bf16[256,256]{1,0:T(8,128)(2,1)S(1)}, bf16[256,256]{1,0:T(8,128)(2,1)}, u32[]{:S(2)}) copy-start(bf16[256,256]{1,0:T(8,128)(2,1)} %param.10) | copy-start | bytes 393220
  12.4 13.4 %copy-start.3 = (bf16[256,256]{1,0:T(8,128)(2,1)S(1)}, bf16[256,256]{1,0:T(8,128)(2,1)}, u32[]{:S(2)}) copy-start(bf16[256,256]{1,0:T(8,128)(2,1)} %param.9) | copy-start | bytes 393220
  12.4 13.4 %copy-start.4 = (bf16[1,256,256]{2,1,0:T(8,128)(2,1)S(1)}, bf16[1,256,256]{2,1,0:T(8,128)(2,1)}, u32[]{:S(2)}) copy-start(bf16[1,256,256]{2,1,0:T(8,128)(2,1)} %param.8) | copy-start | bytes 393220
  12.4 14.5 %copy-start.5 = (s32[1,256,1]{1,2,0:T(1,128)S(1)}, s32[1,256,1]{1,2,0:T(1,128)}, u32[]{:S(2)}) copy-start(s32[1,256,1]{1,2,0:T(1,128)} %param.14) | copy-start | bytes 3076
  12.4 15.4 %copy-start.7 = (s32[1,256]{1,0:T(1,128)S(1)}, s32[1,256]{1,0:T(1,128)}, u32[]{:S(2)}) copy-start(s32[1,256]{1,0:T(1,128)} %param.15) | copy-start | bytes 3076
  12.4 220.3 %all-to-all-start = ((bf16[64,256,256]{2,1,0:T(8,128)(2,1)}), bf16[64,256,256]{2,1,0:T(8,128)(2,1)}, u32[]{:S(2)}, u32[]{:S(2)}) async-start(bf16[64,256,256]{2,1,0:T(8,128)(2,1)} %stack.3), calls=%async_computation | async-start | bytes 16777216 | tf_op jit(solution)/shard_map/all_to_all | solution.py:126
  25.7 334.9 %all-gather.2.cloned.1.call-start = ((), (), s32[]{:S(2)}) async-start(), calls=%async_computation.7 | async-start | bytes 8519680 | tf_op jit(solution)/shard_map/all_gather | solution.py:136
  244.2 8.2 %copy-start.6 = (f32[1,256]{1,0:T(1,128)S(1)}, f32[1,256]{1,0:T(1,128)}, u32[]{:S(2)}) copy-start(f32[1,256]{1,0:T(1,128)} %param.12) | copy-start | bytes 3076
  244.2 8.2 %copy-start.8 = (s32[1,256]{1,0:T(1,128)S(1)}, s32[1,256]{1,0:T(1,128)}, u32[]{:S(2)}) copy-start(s32[1,256]{1,0:T(1,128)} %param.13) | copy-start | bytes 3076
  265.3 95.2 %copy-start.2 = (bf16[1,256,256]{2,1,0:T(8,128)(2,1)S(1)}, bf16[1,256,256]{2,1,0:T(8,128)(2,1)}, u32[]{:S(2)}) copy-start(bf16[1,256,256]{2,1,0:T(8,128)(2,1)} %param.11) | copy-start | bytes 393220
  267.6 17.9 %all-to-all-start.1 = ((f32[8,32,512]{2,1,0:T(8,128)}), f32[8,32,512]{2,1,0:T(8,128)S(1)}, u32[]{:S(2)}, u32[]{:S(2)}) async-start(f32[8,32,512]{2,1,0:T(8,128)} %copy.25), calls=%async_computation.1 | async-start | bytes 1048576 | tf_op jit(solution)/shard_map/all_to_all | solution.py:33
  286.2 50.8 %all-to-all-start.2 = ((f32[32,1,512]{2,1,0:T(1,128)}), f32[32,1,512]{2,1,0:T(1,128)S(1)}, u32[]{:S(2)}, u32[]{:S(2)}) async-start(f32[32,1,512]{2,1,0:T(1,128)} %all_to_all.27), calls=%async_computation.2 | async-start | bytes 131072 | tf_op jit(solution)/shard_map/all_to_all | solution.py:41
  337.7 15.6 %all-to-all-start.3 = ((f32[32,1,512]{2,1,0:T(1,128)}), f32[32,1,512]{2,1,0:T(1,128)S(1)}, u32[]{:S(2)}, u32[]{:S(2)}) async-start(f32[32,1,512]{2,1,0:T(1,128)} %broadcast_in_dim.17), calls=%async_computation.3 | async-start | bytes 131072 | tf_op jit(solution)/shard_map/all_to_all | solution.py:54
  354.0 19.4 %all-to-all-start.5 = ((f32[256,1,16,1]{2,3,1,0:T(1,128)}), f32[256,1,16,1]{2,3,1,0:T(1,128)S(1)}, u32[]{:S(2)}, u32[]{:S(2)}) async-start(f32[256,1,16,1]{2,3,1,0:T(1,128)} %bitcast.15), calls=%async_computation.5 | async-start | bytes 262144 | tf_op jit(solution)/shard_map/all_to_all | solution.py:92
  374.3 21.8 %all-to-all-start.4 = ((f32[8,32,512]{2,1,0:T(8,128)}), f32[8,32,512]{2,1,0:T(8,128)}, u32[]{:S(2)}, u32[]{:S(2)}) async-start(f32[8,32,512]{2,1,0:T(8,128)} %broadcast_in_dim.19), calls=%async_computation.4 | async-start | bytes 1048576 | tf_op jit(solution)/shard_map/all_to_all | solution.py:54
  392.6 76.9 %copy-start.1 = (bf16[256,256]{1,0:T(8,128)(2,1)S(1)}, bf16[256,256]{1,0:T(8,128)(2,1)}, u32[]{:S(2)}) copy-start(bf16[256,256]{1,0:T(8,128)(2,1)} %param.10) | copy-start | bytes 393220
  396.1 43.2 %all-to-all-start.6 = ((f32[256,1,1024]{2,1,0:T(1,128)}), f32[256,1,1024]{2,1,0:T(1,128)S(1)}, u32[]{:S(2)}, u32[]{:S(2)}) async-start(f32[256,1,1024]{2,1,0:T(1,128)} %reshape.207), calls=%async_computation.6 | async-start | bytes 2097152 | tf_op jit(solution)/shard_map/all_to_all | solution.py:92
Sparse Core Ops, SparseCore 0:
  29.8 144.0 all-gather.1
